TPU v7x, 512 devices: a whole 4x4x16 slice. The times are simulated.
512 devices in a mesh: row: 32 (over z_lo, x), col: 16 (over z_hi, y, core).
Axes of the slice: x: 4, y: 4, z: 16 (z_hi: 2, z_lo: 8; z = z_hi * 8 + z_lo), core: 2. Of those that a mesh axis runs over, the one named last changes fastest.
Arguments:
- noisy: float32 [1024, 32768], P('row', 'col'), may hold values from -9 to 9
Outputs:
- denoised: float32 [1024, 32768], P('row', 'col')
- gap: float32 [4], replicated
All inputs are finite; a program needn't handle non-finite values.
Results may differ from a plain program's by a relative error of at most 0.0003.
Values sent between devices are 32-bit elements; how exact they have to be, the bound alone decides.
A program may use at most 64 MiB of HBM per device.

v0:
```python
import jax
import jax.numpy as jnp
from jax import lax
from jax.sharding import Mesh
from jax.sharding import PartitionSpec as P

ITERS = 4
ROW = ("row_0", "row_1")
COL = ("col_0", "col_1", "col_2")
ROW_COL = ("row_0", "row_1", "col_0", "col_1", "col_2")
fidelity = 8.0
primal_step = 0.35
dual_step = 0.35


def with_halo(shard, sides, width):
    for axis, dim in sides:
        size, length = (lax.axis_size(axis), shard.shape[dim])
        up = [(i, (i + 1) % size) for i in range(size - 1)]
        down = [(j, i) for i, j in up]
        last = lax.slice_in_dim(shard, length - width, length, axis=dim)
        first = lax.slice_in_dim(shard, 0, width, axis=dim)
        before = lax.ppermute(last, axis, up)
        after = lax.ppermute(first, axis, down)
        shard = jnp.concatenate([before, shard, after], axis=dim)
    return shard


def by_axis(shard, axes):
    for axis in axes:
        shard = lax.psum(shard, axis)
    return shard


def gap_piece(edge_rows, edge_cols, primal, noisy, diverged):
    return jnp.sum(jnp.sqrt(edge_rows * edge_rows + edge_cols * edge_cols)) + jnp.sum(
        0.5 * fidelity * (primal - noisy) ** 2
        + noisy * diverged
        + diverged * diverged / (2.0 * fidelity)
    )


def deep_run(noisy):
    tile_rows, tile_cols = noisy.shape
    rows_all = lax.axis_size(ROW) * tile_rows
    cols_all = lax.axis_size(COL) * tile_cols
    margin = ITERS + 1
    framed = with_halo(noisy, ((ROW, 0), (COL, 1)), margin)
    global_rows = (
        lax.axis_index(ROW) * tile_rows
        - margin
        + jnp.arange(tile_rows + 2 * margin, dtype=jnp.int32)
    )
    global_cols = (
        lax.axis_index(COL) * tile_cols
        - margin
        + jnp.arange(tile_cols + 2 * margin, dtype=jnp.int32)
    )
    rows_inside = (global_rows >= 0) & (global_rows < rows_all)
    rows_inner = (global_rows >= 0) & (global_rows < rows_all - 1)
    cols_inside = (global_cols >= 0) & (global_cols < cols_all)
    cols_inner = (global_cols >= 0) & (global_cols < cols_all - 1)
    mask_rows = (rows_inner[:, None] & cols_inside[None, :]).astype(jnp.float32)
    mask_cols = (rows_inside[:, None] & cols_inner[None, :]).astype(jnp.float32)
    frame_rows, frame_cols = framed.shape

    def masked_grads(field):
        row_diff = jnp.concatenate(
            [field[1:] - field[:-1], jnp.zeros((1, frame_cols), jnp.float32)], 0
        )
        col_diff = jnp.concatenate(
            [field[:, 1:] - field[:, :-1], jnp.zeros((frame_rows, 1), jnp.float32)], 1
        )
        return (row_diff * mask_rows, col_diff * mask_cols)

    primal = framed
    previous = framed
    dual = jnp.zeros((2,) + framed.shape, jnp.float32)
    pieces = []
    for iteration in range(ITERS):
        extrapolated = 2.0 * primal - previous
        grad_rows, grad_cols = masked_grads(extrapolated)
        trial = dual + dual_step * jnp.stack([grad_rows, grad_cols])
        shrink = 1.0 / jnp.maximum(1.0, jnp.sqrt(trial[0] * trial[0] + trial[1] * trial[1]))
        dual = trial * shrink
        diverged = (
            dual[0]
            - jnp.concatenate([jnp.zeros((1, frame_cols), jnp.float32), dual[0, :-1]], 0)
            + dual[1]
            - jnp.concatenate([jnp.zeros((frame_rows, 1), jnp.float32), dual[1, :, :-1]], 1)
        )
        updated = (primal + primal_step * diverged + primal_step * fidelity * framed) / (
            1.0 + primal_step * fidelity
        )
        previous = primal
        primal = updated
        edge_rows, edge_cols = masked_grads(primal)
        owned_r = slice(margin, margin + tile_rows)
        owned_c = slice(margin, margin + tile_cols)
        pieces.append(
            gap_piece(
                edge_rows[owned_r, owned_c],
                edge_cols[owned_r, owned_c],
                primal[owned_r, owned_c],
                noisy,
                diverged[owned_r, owned_c],
            )
        )
    return (primal[margin : margin + tile_rows, margin : margin + tile_cols], pieces)


def on_device(noisy):
    cells = lax.axis_size(ROW) * noisy.shape[0] * lax.axis_size(COL) * noisy.shape[1]
    primal, pieces = deep_run(noisy)
    gap = by_axis(jnp.stack(pieces), ROW_COL) / cells
    return (primal, gap)


def solution(mesh):
    torus = Mesh(mesh.devices.reshape(8, 4, 2, 4, 2), ("row_0", "row_1", "col_0", "col_1", "col_2"))
    return jax.shard_map(
        on_device,
        mesh=torus,
        in_specs=(P(ROW, COL),),
        out_specs=(P(ROW, COL), P()),
        check_vma=False,
    )
```

profile of v0, /device:TPU:1, one launch (start us, length us, event | category | flops | bytes accessed | tf_op | source)
XLA Modules:
  0.0 118.6 jit_solution(13011369884884892752)
XLA Ops:
  0.6 0.9 fusion.92
  1.6 1.3 %collective-permute-start.1 = (f32[5,2048]{1,0:T(8,128)S(1)}, f32[5,2048]{1,0:T(8,128)S(1)}, u32[]{:S(2)}, u32[]{:S(2)}) collective-permute-start(f32[5,2048]{1,0:T(8,128)S(1)} %get-tuple-element.24), channel_id=1, source_target_pairs={{16,0},{32,16},{48,32},{64,48},{80,64},{96,80},{112,96},{128,112},... | collective-permute-start | bytes 122888 | tf_op jit(solution)/shard_map/ppermute | solution.py:24
  2.9 4.6 %collective-permute-start = (f32[5,2048]{1,0:T(8,128)S(1)}, f32[5,2048]{1,0:T(8,128)S(1)}, u32[]{:S(2)}, u32[]{:S(2)}) collective-permute-start(f32[5,2048]{1,0:T(8,128)S(1)} %get-tuple-element.23), channel_id=1, source_target_pairs={{0,16},{16,32},{32,48},{48,64},{64,80},{80,96},{96,112},{112,128},... | collective-permute-start | bytes 122888 | tf_op jit(solution)/shard_map/ppermute | solution.py:23
  7.6 1.1 collective-permute-done
  8.9 5.1 %collective-permute-start.2 = (f32[42,5]{1,0:T(8,128)S(1)}, f32[42,5]{1,0:T(8,128)S(1)}, u32[]{:S(2)}, u32[]{:S(2)}) collective-permute-start(f32[42,5]{1,0:T(8,128)S(1)} %get-tuple-element.22), channel_id=1, source_target_pairs={{0,1},{1,2},{2,3},{3,4},{4,5},{5,6},{6,7},{7,8},{8,9},{9,10},{10,1... | collective-permute-start | bytes 2528 | tf_op jit(solution)/shard_map/ppermute | solution.py:23
  14.0 5.5 %collective-permute-start.3 = (f32[42,5]{1,0:T(8,128)S(1)}, f32[42,5]{1,0:T(8,128)S(1)}, u32[]{:S(2)}, u32[]{:S(2)}) collective-permute-start(f32[42,5]{1,0:T(8,128)S(1)} %get-tuple-element.21), channel_id=1, source_target_pairs={{1,0},{2,1},{3,2},{4,3},{5,4},{6,5},{7,6},{8,7},{9,8},{10,9},{11,1... | collective-permute-start | bytes 2528 | tf_op jit(solution)/shard_map/ppermute | solution.py:24
  19.6 0.7 collective-permute-done.3
  20.3 0.3 concatenate.79
  21.5 0.2 fusion.46
  22.9 0.3 multiply_subtract_fusion.2
  23.7 0.2 fusion.1
  24.1 0.3 broadcast_multiply_fusion.1
  24.5 0.4 multiply_subtract_fusion.1
  25.3 0.3 fusion.2
  25.8 0.4 broadcast_multiply_fusion
  26.7 0.3 add_multiply_fusion
  27.5 2.0 %fusion.76 = (f32[]{:T(128)}, f32[]{:T(128)}, f32[]{:T(128)}, f32[]{:T(128)}, f32[32,2048]{1,0:T(8,128)}) fusion(f32[32,2048]{1,0:T(8,128)S(1)} %copy-done, f32[42,2058]{1,0:T(8,128)S(1)} %get-tuple-element.11, f32[42,2058]{1,0:T(8,128)S(1)} %get-tuple-element.12, f32[42,2058]{1,0:T(8,128)S(1)} %get-tuple-element.20, f32[42,2058]{1,0:T(8,128)S(1)} %get-tuple-element.18, ...), kind=kLoop, calls=%fused_computation.149 | loop fusion | flops 2359292 | bytes 2621456 | tf_op jit(solution)/shard_map/reduce_sum | solution.py:36
  29.5 1.6 %fusion.80 = (f32[]{:T(128)}, f32[]{:T(128)}, f32[]{:T(128)}, f32[]{:T(128)}) fusion(f32[42,2057]{1,0:T(8,128)S(1)} %slice_subtract_fusion.6, f32[41,2058]{1,0:T(8,128)S(1)} %slice_subtract_fusion.7, pred[42,2058]{1,0:T(8,128)(4,1)S(1)} %broadcast_and_fusion, pred[42,2058]{1,0:T(8,128)(4,1)S(1)} %broadcast_and_fusion.1, ...), kind=kLoop, calls=%fused_computation.154 | loop fusion | flops 1572860 | bytes 2863440 | tf_op jit(solution)/shard_map/reduce_sum | solution.py:36
  36.3 36.1 %psum.35 = f32[4]{0:T(128)S(1)} all-reduce(f32[4]{0:T(128)S(1)} %pad_maximum_fusion.2), channel_id=1, replica_groups=mesh['row_0'=8,'row_1'=4,'col_0'=2,'col_1'=4,'col_2'=2] {'row_0'}, use_global_device_ids=true, to_apply=%region_8.0 | all-reduce | flops 4 | bytes 32 | tf_op jit(solution)/shard_map/psum | solution.py:31
  72.4 6.0 %psum.36 = f32[4]{0:T(128)S(1)} all-reduce(f32[4]{0:T(128)S(1)} %psum.35), channel_id=1, replica_groups=mesh['row_0'=8,'row_1'=4,'col_0'=2,'col_1'=4,'col_2'=2] {'row_1'}, use_global_device_ids=true, to_apply=%region_9.0 | all-reduce | flops 4 | bytes 32 | tf_op jit(solution)/shard_map/psum | solution.py:31
  78.3 12.5 %psum.37 = f32[4]{0:T(128)S(1)} all-reduce(f32[4]{0:T(128)S(1)} %psum.36), channel_id=1, replica_groups=mesh['row_0'=8,'row_1'=4,'col_0'=2,'col_1'=4,'col_2'=2] {'col_0'}, use_global_device_ids=true, to_apply=%region_10.0 | all-reduce | flops 4 | bytes 32 | tf_op jit(solution)/shard_map/psum | solution.py:31
  90.8 24.8 %psum.38 = f32[4]{0:T(128)S(1)} all-reduce(f32[4]{0:T(128)S(1)} %psum.37), channel_id=1, replica_groups=mesh['row_0'=8,'row_1'=4,'col_0'=2,'col_1'=4,'col_2'=2] {'col_1'}, use_global_device_ids=true, to_apply=%region_11.0 | all-reduce | flops 4 | bytes 32 | tf_op jit(solution)/shard_map/psum | solution.py:31
  115.6 2.5 %psum.39 = f32[4]{0:T(128)S(1)} all-reduce(f32[4]{0:T(128)S(1)} %psum.38), channel_id=1, replica_groups=mesh['row_0'=8,'row_1'=4,'col_0'=2,'col_1'=4,'col_2'=2] {'col_2'}, use_global_device_ids=true, to_apply=%region_12.0 | all-reduce | flops 4 | bytes 32 | tf_op jit(solution)/shard_map/psum | solution.py:31
  118.1 0.5 broadcast_multiply_fusion.5
  (53 shorter events, 4.7 us)
Async XLA Ops:
  0.6 8.1 %copy-start = (f32[32,2048]{1,0:T(8,128)S(1)}, f32[32,2048]{1,0:T(8,128)}, u32[]{:S(2)}) copy-start(f32[32,2048]{1,0:T(8,128)} %param.1) | copy-start | bytes 786436
  1.6 6.0 %collective-permute-start.1 = (f32[5,2048]{1,0:T(8,128)S(1)}, f32[5,2048]{1,0:T(8,128)S(1)}, u32[]{:S(2)}, u32[]{:S(2)}) collective-permute-start(f32[5,2048]{1,0:T(8,128)S(1)} %get-tuple-element.24), channel_id=1, source_target_pairs={{16,0},{32,16},{48,32},{64,48},{80,64},{96,80},{112,96},{128,112},... | collective-permute-start | bytes 122888 | tf_op jit(solution)/shard_map/ppermute | solution.py:24
  2.9 5.9 %collective-permute-start = (f32[5,2048]{1,0:T(8,128)S(1)}, f32[5,2048]{1,0:T(8,128)S(1)}, u32[]{:S(2)}, u32[]{:S(2)}) collective-permute-start(f32[5,2048]{1,0:T(8,128)S(1)} %get-tuple-element.23), channel_id=1, source_target_pairs={{0,16},{16,32},{32,48},{48,64},{64,80},{80,96},{96,112},{112,128},... | collective-permute-start | bytes 122888 | tf_op jit(solution)/shard_map/ppermute | solution.py:23
  8.9 10.7 %collective-permute-start.2 = (f32[42,5]{1,0:T(8,128)S(1)}, f32[42,5]{1,0:T(8,128)S(1)}, u32[]{:S(2)}, u32[]{:S(2)}) collective-permute-start(f32[42,5]{1,0:T(8,128)S(1)} %get-tuple-element.22), channel_id=1, source_target_pairs={{0,1},{1,2},{2,3},{3,4},{4,5},{5,6},{6,7},{7,8},{8,9},{9,10},{10,1... | collective-permute-start | bytes 2528 | tf_op jit(solution)/shard_map/ppermute | solution.py:23
  14.0 6.3 %collective-permute-start.3 = (f32[42,5]{1,0:T(8,128)S(1)}, f32[42,5]{1,0:T(8,128)S(1)}, u32[]{:S(2)}, u32[]{:S(2)}) collective-permute-start(f32[42,5]{1,0:T(8,128)S(1)} %get-tuple-element.21), channel_id=1, source_target_pairs={{1,0},{2,1},{3,2},{4,3},{5,4},{6,5},{7,6},{8,7},{9,8},{10,9},{11,1... | collective-permute-start | bytes 2528 | tf_op jit(solution)/shard_map/ppermute | solution.py:24
where the time goes:
time: 119 us
  blocking collectives  81.8 us (69%)
  starting transfers between devices  16.4 us (14%)
  other arithmetic  11 us (9%)
  between operations  6.05 us (5%)
  waiting for transfers between devices  1.83 us (2%)
  local copies, waits for them, and re-layouts  1.49 us (1%)
    psum x5, blocking collectives, by_axis(): shard = lax.psum(shard, axis)  81.8 us
    ppermute x2, starting transfers between devices, with_halo(): before = lax.ppermute(last, axis, up)  9.7 us
    ppermute x2, starting transfers between devices, with_halo(): after = lax.ppermute(first, axis, down)  6.75 us
  transfers between devices with their start and end apart: 4, of which 2 were waited for; matrix products, arithmetic and copies ran while one was open for 0% of the time, Pallas kernels for 0%

commit v1 on v0

--- a/solution.py
+++ b/solution.py
@@ -28,7 +28,8 @@
 
 def by_axis(shard, axes):
     for axis in axes:
-        shard = lax.psum(shard, axis)
+        reach_grid = lambda xx, axis_id: jnp.sum(jax.lax.all_gather(xx, axis_name=axis_id), axis=0)
+        shard = reach_grid(shard, axis_id=axis)
     return shard
 
 

time: 119 us -> 124 us (1.042)
  local copies, waits for them, and re-layouts: 1.49 us -> 9.28 us
  blocking collectives: 81.8 us -> 76.5 us
  between operations: 6.05 us -> 9.36 us
    psum x5 -> x0, blocking collectives: 81.8 us -> none  [by_axis(): shard = lax.psum(shard, axis)]
    unnamed x0 -> x5, blocking collectives: none -> 76.5 us
    unnamed x2 -> x16, local copies, waits for them, and re-layouts: 0.01 us -> 7.38 us
  transfers between devices with their start and end apart: 4 -> 4, of which waited for: 2 -> 1; matrix products, arithmetic and copies ran while one was open for 0% -> 5% of each run, Pallas kernels for 0% -> 0%
where the time goes in v1:
time: 124 us
  blocking collectives  76.5 us (62%)
  starting transfers between devices  16.4 us (13%)
  other arithmetic  11.2 us (9%)
  between operations  9.36 us (8%)
  local copies, waits for them, and re-layouts  9.28 us (7%)
    unnamed x5, blocking collectives  76.5 us
    ppermute x2, starting transfers between devices, with_halo(): before = lax.ppermute(last, axis, up)  9.7 us
    unnamed x16, local copies, waits for them, and re-layouts  7.38 us
    ppermute x2, starting transfers between devices, with_halo(): after = lax.ppermute(first, axis, down)  6.75 us
  transfers between devices with their start and end apart: 4, of which 1 were waited for; matrix products, arithmetic and copies ran while one was open for 5% of the time, Pallas kernels for 0%

profile of v1, /device:TPU:1, one launch (start us, length us, event | category | flops | bytes accessed | tf_op | source)
XLA Modules:
  0.0 123.8 jit_solution(707944269575873974)
XLA Ops:
  0.6 0.9 fusion.92
  1.6 1.3 %collective-permute-start.1 = (f32[5,2048]{1,0:T(8,128)S(1)}, f32[5,2048]{1,0:T(8,128)S(1)}, u32[]{:S(2)}, u32[]{:S(2)}) collective-permute-start(f32[5,2048]{1,0:T(8,128)S(1)} %get-tuple-element.24), channel_id=1, source_target_pairs={{16,0},{32,16},{48,32},{64,48},{80,64},{96,80},{112,96},{128,112},... | collective-permute-start | bytes 122888 | tf_op jit(solution)/shard_map/ppermute | solution.py:24
  2.9 4.6 %collective-permute-start = (f32[5,2048]{1,0:T(8,128)S(1)}, f32[5,2048]{1,0:T(8,128)S(1)}, u32[]{:S(2)}, u32[]{:S(2)}) collective-permute-start(f32[5,2048]{1,0:T(8,128)S(1)} %get-tuple-element.23), channel_id=1, source_target_pairs={{0,16},{16,32},{32,48},{48,64},{64,80},{80,96},{96,112},{112,128},... | collective-permute-start | bytes 122888 | tf_op jit(solution)/shard_map/ppermute | solution.py:23
  7.8 1.0 collective-permute-done
  8.9 5.1 %collective-permute-start.2 = (f32[42,5]{1,0:T(8,128)S(1)}, f32[42,5]{1,0:T(8,128)S(1)}, u32[]{:S(2)}, u32[]{:S(2)}) collective-permute-start(f32[42,5]{1,0:T(8,128)S(1)} %get-tuple-element.22), channel_id=1, source_target_pairs={{0,1},{1,2},{2,3},{3,4},{4,5},{5,6},{6,7},{7,8},{8,9},{9,10},{10,1... | collective-permute-start | bytes 2528 | tf_op jit(solution)/shard_map/ppermute | solution.py:23
  14.0 5.5 %collective-permute-start.3 = (f32[42,5]{1,0:T(8,128)S(1)}, f32[42,5]{1,0:T(8,128)S(1)}, u32[]{:S(2)}, u32[]{:S(2)}) collective-permute-start(f32[42,5]{1,0:T(8,128)S(1)} %get-tuple-element.21), channel_id=1, source_target_pairs={{1,0},{2,1},{3,2},{4,3},{5,4},{6,5},{7,6},{8,7},{9,8},{10,9},{11,1... | collective-permute-start | bytes 2528 | tf_op jit(solution)/shard_map/ppermute | solution.py:24
  19.5 1.3 %dynamic-slice = u32[1]{0:T(128)} dynamic-slice(u32[512]{0:T(512)} %constant.145, u32[]{:T(128)S(6)} %add.236), dynamic_slice_sizes={1} | dynamic-slice | bytes 12
  20.8 1.3 %dynamic-slice.1 = u32[1]{0:T(128)} dynamic-slice(u32[512]{0:T(512)} %constant.150, u32[]{:T(128)S(6)} %add.236), dynamic_slice_sizes={1} | dynamic-slice | bytes 12
  23.3 1.3 %dynamic-slice.2 = u32[1]{0:T(128)} dynamic-slice(u32[512]{0:T(512)} %constant.155, u32[]{:T(128)S(6)} %add.236), dynamic_slice_sizes={1} | dynamic-slice | bytes 12
  25.2 1.3 %dynamic-slice.3 = u32[1]{0:T(128)} dynamic-slice(u32[512]{0:T(512)} %constant.160, u32[]{:T(128)S(6)} %add.236), dynamic_slice_sizes={1} | dynamic-slice | bytes 12
  27.2 1.3 %dynamic-slice.4 = u32[1]{0:T(128)} dynamic-slice(u32[512]{0:T(512)} %constant.165, u32[]{:T(128)S(6)} %add.236), dynamic_slice_sizes={1} | dynamic-slice | bytes 12
  31.1 0.3 multiply_subtract_fusion.2
  32.7 0.4 multiply_subtract_fusion.1
  33.5 0.3 fusion.2
  34.0 0.4 broadcast_multiply_fusion
  34.9 0.3 add_multiply_fusion
  35.7 2.0 %fusion.76 = (f32[]{:T(128)}, f32[]{:T(128)}, f32[]{:T(128)}, f32[]{:T(128)}, f32[32,2048]{1,0:T(8,128)}) fusion(f32[32,2048]{1,0:T(8,128)S(1)} %copy-done, f32[42,2058]{1,0:T(8,128)S(1)} %get-tuple-element.11, f32[42,2058]{1,0:T(8,128)S(1)} %get-tuple-element.12, f32[42,2058]{1,0:T(8,128)S(1)} %get-tuple-element.20, f32[42,2058]{1,0:T(8,128)S(1)} %get-tuple-element.18, ...), kind=kLoop, calls=%fused_computation.149 | loop fusion | flops 2359292 | bytes 2621456 | tf_op jit(solution)/shard_map/reduce_sum | solution.py:37
  37.7 1.6 %fusion.80 = (f32[]{:T(128)}, f32[]{:T(128)}, f32[]{:T(128)}, f32[]{:T(128)}) fusion(f32[42,2057]{1,0:T(8,128)S(1)} %slice_subtract_fusion.6, f32[41,2058]{1,0:T(8,128)S(1)} %slice_subtract_fusion.7, pred[42,2058]{1,0:T(8,128)(4,1)S(1)} %broadcast_and_fusion, pred[42,2058]{1,0:T(8,128)(4,1)S(1)} %broadcast_and_fusion.1, ...), kind=kLoop, calls=%fused_computation.154 | loop fusion | flops 1572860 | bytes 2863440 | tf_op jit(solution)/shard_map/reduce_sum | solution.py:37
  44.6 33.8 %all-reduce.24 = f32[32]{0:T(128)S(1)} all-reduce(f32[32]{0:T(128)S(1)} %maximum_dynamic-update-slice_fusion), channel_id=2, replica_groups=mesh['row_0'=8,'row_1'=4,'col_0'=2,'col_1'=4,'col_2'=2] {'row_0'}, use_global_device_ids=true, to_apply=%add.24 | all-reduce | flops 32 | bytes 256
  78.7 6.0 %all-reduce.25 = f32[16]{0:T(128)S(1)} all-reduce(f32[16]{0:T(128)S(1)} %dynamic-update-slice.1), channel_id=3, replica_groups=mesh['row_0'=8,'row_1'=4,'col_0'=2,'col_1'=4,'col_2'=2] {'row_1'}, use_global_device_ids=true, to_apply=%add.25 | all-reduce | flops 16 | bytes 128
  85.7 12.5 %all-reduce.26 = f32[8]{0:T(128)S(1)} all-reduce(f32[8]{0:T(128)S(1)} %dynamic-update-slice.2), channel_id=4, replica_groups=mesh['row_0'=8,'row_1'=4,'col_0'=2,'col_1'=4,'col_2'=2] {'col_0'}, use_global_device_ids=true, to_apply=%add.26 | all-reduce | flops 8 | bytes 64
  98.5 18.9 %all-reduce.27 = f32[16]{0:T(128)S(1)} all-reduce(f32[16]{0:T(128)S(1)} %dynamic-update-slice.3), channel_id=5, replica_groups=mesh['row_0'=8,'row_1'=4,'col_0'=2,'col_1'=4,'col_2'=2] {'col_1'}, use_global_device_ids=true, to_apply=%add.27 | all-reduce | flops 16 | bytes 128
  117.8 5.3 %all-reduce.28 = f32[8]{0:T(128)S(1)} all-reduce(f32[8]{0:T(128)S(1)} %dynamic-update-slice.4), channel_id=6, replica_groups=mesh['row_0'=8,'row_1'=4,'col_0'=2,'col_1'=4,'col_2'=2] {'col_2'}, use_global_device_ids=true, to_apply=%add.28 | all-reduce | flops 8 | bytes 64
  123.3 0.5 broadcast_multiply_fusion.5
  (77 shorter events, 7.3 us)
Async XLA Ops:
  0.6 8.1 %copy-start = (f32[32,2048]{1,0:T(8,128)S(1)}, f32[32,2048]{1,0:T(8,128)}, u32[]{:S(2)}) copy-start(f32[32,2048]{1,0:T(8,128)} %param.1) | copy-start | bytes 786436
  1.6 6.2 %collective-permute-start.1 = (f32[5,2048]{1,0:T(8,128)S(1)}, f32[5,2048]{1,0:T(8,128)S(1)}, u32[]{:S(2)}, u32[]{:S(2)}) collective-permute-start(f32[5,2048]{1,0:T(8,128)S(1)} %get-tuple-element.24), channel_id=1, source_target_pairs={{16,0},{32,16},{48,32},{64,48},{80,64},{96,80},{112,96},{128,112},... | collective-permute-start | bytes 122888 | tf_op jit(solution)/shard_map/ppermute | solution.py:24
  2.9 5.9 %collective-permute-start = (f32[5,2048]{1,0:T(8,128)S(1)}, f32[5,2048]{1,0:T(8,128)S(1)}, u32[]{:S(2)}, u32[]{:S(2)}) collective-permute-start(f32[5,2048]{1,0:T(8,128)S(1)} %get-tuple-element.23), channel_id=1, source_target_pairs={{0,16},{16,32},{32,48},{48,64},{64,80},{80,96},{96,112},{112,128},... | collective-permute-start | bytes 122888 | tf_op jit(solution)/shard_map/ppermute | solution.py:23
  8.9 19.6 %collective-permute-start.2 = (f32[42,5]{1,0:T(8,128)S(1)}, f32[42,5]{1,0:T(8,128)S(1)}, u32[]{:S(2)}, u32[]{:S(2)}) collective-permute-start(f32[42,5]{1,0:T(8,128)S(1)} %get-tuple-element.22), channel_id=1, source_target_pairs={{0,1},{1,2},{2,3},{3,4},{4,5},{5,6},{6,7},{7,8},{8,9},{9,10},{10,1... | collective-permute-start | bytes 2528 | tf_op jit(solution)/shard_map/ppermute | solution.py:23
  14.0 14.5 %collective-permute-start.3 = (f32[42,5]{1,0:T(8,128)S(1)}, f32[42,5]{1,0:T(8,128)S(1)}, u32[]{:S(2)}, u32[]{:S(2)}) collective-permute-start(f32[42,5]{1,0:T(8,128)S(1)} %get-tuple-element.21), channel_id=1, source_target_pairs={{1,0},{2,1},{3,2},{4,3},{5,4},{6,5},{7,6},{8,7},{9,8},{10,9},{11,1... | collective-permute-start | bytes 2528 | tf_op jit(solution)/shard_map/ppermute | solution.py:24
